TPU v7x, 32 devices: a whole 2x2x4 slice. The times are simulated.
32 devices in a mesh: gx: 8 (over z, x), gy: 4 (over y, core).
Axes of the slice: x: 2, y: 2, z: 4, core: 2. Of those that a mesh axis runs over, the one named last changes fastest.
Arguments:
- orbitals: bfloat16 [20000, 200], P('gx'), may hold values from -6 to 6
- projector: bfloat16 [6016, 20000], P('gy', 'gx'), may hold values from -0.0390625 to 0.0390625
- integrals: bfloat16 [8, 6016, 6016], P('gx', 'gy'), may hold values from -1 to 1
Outputs:
- exchange_matrix: float32 [6016, 6016], P('gx', 'gy')
- exchange_orbitals: float32 [20000, 200], P('gx', 'gy')
- energy_mean: float32 [], replicated
- trace_mean: float32 [], replicated
All inputs are finite; a program needn't handle non-finite values.
Results may differ from a plain program's by a relative error of at most 0.008.
Values may be sent and summed in bfloat16 or wider, within the bound.
A program may use at most 128 MiB of HBM per device.

v0:
```python
import jax
import jax.numpy as jnp
from jax import lax
from jax.sharding import PartitionSpec as P


def spread(block, axis, holder):
    block = jnp.where(lax.axis_index(axis) == holder, block, jnp.zeros_like(block))
    return lax.psum(block, axis)


def on_device(orbitals, projector, integrals):
    part_rows = projector.shape[0]
    partial_value = jnp.dot(projector, orbitals, preferred_element_type=jnp.float32)
    own_admm = lax.psum(partial_value, "gx").astype(jnp.bfloat16)
    admm = lax.all_gather(own_admm, "gy", axis=0, tiled=True)
    half = lax.dot_general(
        integrals, admm, (((2,), (0,)), ((), ())), preferred_element_type=jnp.float32
    ).astype(jnp.bfloat16)
    size_x = lax.axis_size("gx")
    block_rows = admm.shape[0] // size_x
    index_x = lax.axis_index("gx")
    index_y = lax.axis_index("gy")
    all_half = lax.all_gather(half, "gx", axis=0, tiled=True)
    first_row = index_x * block_rows
    root = first_row // part_rows
    offset = jnp.clip(first_row - index_y * part_rows, 0, part_rows - block_rows)
    mine = lax.dynamic_slice_in_dim(all_half, offset, block_rows, 1)
    columns = spread(mine, "gy", root)
    exchange = lax.dot_general(
        columns, all_half, (((0, 2), (0, 2)), ((), ())), preferred_element_type=jnp.float32
    )
    row_ids = index_x * block_rows + lax.iota(jnp.int32, block_rows)
    col_ids = index_y * part_rows + lax.iota(jnp.int32, part_rows)
    diag_mask = row_ids[:, None] == col_ids[None, :]
    trace_part = jnp.sum(jnp.where(diag_mask, exchange, 0.0))
    trace_total = lax.psum(trace_part, ("gx", "gy"))
    admm_wide = admm.astype(jnp.float32)
    col_orbs = lax.dynamic_slice_in_dim(admm_wide, index_x * block_rows, block_rows, 0)
    row_orbs = lax.dynamic_slice_in_dim(admm_wide, index_y * part_rows, part_rows, 0)
    applied_part = lax.dot_general(
        exchange,
        col_orbs,
        (((0,), (0,)), ((), ())),
        precision=lax.Precision.HIGHEST,
        preferred_element_type=jnp.float32,
    )
    energy_part = jnp.sum(row_orbs * applied_part)
    energy_total = lax.psum(energy_part, ("gx", "gy"))
    applied = lax.psum(applied_part, "gx")
    applied_low = applied.astype(jnp.bfloat16)
    back_part = lax.dot_general(
        projector, applied_low, (((0,), (0,)), ((), ())), preferred_element_type=jnp.float32
    )
    back = lax.psum_scatter(back_part, "gy", scatter_dimension=1, tiled=True)
    total_adm = admm.shape[0]
    energy_mean = -0.5 * energy_total / (total_adm * admm.shape[1])
    trace_mean = trace_total / total_adm
    return (exchange, back, energy_mean, trace_mean)


def solution(mesh):
    return jax.shard_map(
        on_device,
        mesh=mesh,
        in_specs=(P("gx", None), P("gy", "gx"), P("gx", "gy", None)),
        out_specs=(P("gx", "gy"), P("gx", "gy"), P(), P()),
        check_vma=False,
    )
```

profile of v0, /device:TPU:7, one launch (start us, length us, event | category | flops | bytes accessed | tf_op | source)
XLA Modules:
  0.0 444.6 jit_solution(2069144303628339878)
XLA Ops:
  7.2 0.0 copy-start
  7.2 0.0 all-gather.6.cloned.1.call-start
  7.2 1.2 copy-done
  8.4 4.9 %fusion.13 = f32[1504,200]{0,1:T(8,128)S(1)} fusion(bf16[1504,2500]{0,1:T(8,128)(2,1)} %param.4, bf16[2500,200]{0,1:T(8,128)(2,1)S(1)} %copy-done), kind=kOutput, calls=%fused_computation.17 | convolution fusion | flops 1504000000 | bytes 9723200 | tf_op jit(solution)/shard_map/dot_general | solution.py:14
  13.3 60.9 %all-reduce.8 = bf16[1504,200]{0,1:T(8,128)(2,1)} all-reduce(f32[1504,200]{0,1:T(8,128)S(1)} %fusion.13), channel_id=1, replica_groups=mesh['gx'=8,'gy'=4] {'gx'}, use_global_device_ids=true, to_apply=%region_0.0 | all-reduce | flops 300800 | bytes 1804800 | tf_op jit(solution)/shard_map/psum | solution.py:15
  74.2 0.0 all-gather.6.cloned.1.call-update
  74.2 0.0 all-gather.8.cloned.1.call-start
  74.3 36.3 %all-gather.6.cloned.1.call-done = bf16[4,1504,200]{1,2,0:T(8,128)(2,1)} async-done(((bf16[1,1504,200]{1,2,0:T(8,128)(2,1)}), bf16[4,1504,200]{1,2,0:T(8,128)(2,1)}) %all-gather.6.cloned.1.call-update) | async-done | bytes 2406416 | tf_op jit(solution)/shard_map/all_gather | solution.py:16
  110.6 3.0 copy.8
  113.5 4.4 reshape.24
  117.9 13.3 %fusion.6 = bf16[1,1504,200]{1,2,0:T(8,128)(2,1)} fusion(bf16[6016,200]{0,1:T(8,128)(2,1)} %reshape.24, bf16[1,1504,6016]{2,1,0:T(8,128)(2,1)} %param.5), kind=kOutput, calls=%fused_computation.7 | convolution fusion | flops 3619526400 | bytes 21104128 | tf_op jit(solution)/shard_map/dot_general | solution.py:17
  131.2 0.0 all-gather.8.cloned.1.call-update
  131.3 0.2 all-reduce.7.cloned.1.call-start
  131.5 79.8 %all-gather.8.cloned.1.call-done = bf16[8,1504,200]{1,2,0:T(8,128)(2,1)} async-done(((bf16[1,1504,200]{1,2,0:T(8,128)(2,1)}), bf16[8,1504,200]{1,2,0:T(8,128)(2,1)}) %all-gather.8.cloned.1.call-update) | async-done | bytes 4812816 | tf_op jit(solution)/shard_map/all_gather | solution.py:24
  211.4 4.8 %dynamic-slice_select_fusion = bf16[8,752,200]{1,2,0:T(8,128)(2,1)} fusion(bf16[8,1504,200]{1,2,0:T(8,128)(2,1)} %all-gather.8.cloned.1.call-done, s32[]{:T(128)S(6)} %min.4, pred[]{:T(512)S(6)} %eq.16), kind=kLoop, calls=%fused_computation.6 | loop fusion | flops 1203200 | bytes 4812805 | tf_op jit(solution)/shard_map/jit(_where)/select_n | solution.py:8
  216.2 0.0 all-reduce.7.cloned.1.call-update
  216.2 57.1 %all-reduce.7.cloned.1.call-done = bf16[8,752,200]{1,2,0:T(8,128)(2,1)} async-done(((bf16[8,752,200]{1,2,0:T(8,128)(2,1)}), bf16[8,752,200]{1,2,0:T(8,128)(2,1)}) %all-reduce.7.cloned.1.call-update) | async-done | bytes 2406416 | tf_op jit(solution)/shard_map/psum | solution.py:9
  273.4 8.2 %select_reduce_fusion = (f32[]{:T(128)}, f32[752,1504]{1,0:T(8,128)S(1)}) fusion(s32[1504]{0:T(1024)S(1)} %iota_add_fusion, s32[752]{0:T(1024)S(1)} %iota_add_fusion.1, bf16[8,752,200]{1,2,0:T(8,128)(2,1)} %all-reduce.7.cloned.1.call-done, bf16[8,1504,200]{1,2,0:T(8,128)(2,1)} %all-gather.8.cloned.1.call-done), kind=kOutput, calls=%fused_computation.2 | convolution fusion | flops 3622618624 | bytes 11752260 | tf_op jit(solution)/shard_map/dot_general | solution.py:30
  281.5 0.0 copy-start.1
  281.5 5.0 %multiply_reduce_fusion = (f32[]{:T(128)}, f32[1504,200]{0,1:T(8,128)S(1)}) fusion(bf16[6016,200]{0,1:T(8,128)(2,1)} %reshape.24, s32[]{:T(128)S(6)} %select_n.28, f32[752,1504]{1,0:T(8,128)S(1)} %get-tuple-element.9, s32[]{:T(128)S(6)} %select_n.27), kind=kOutput, calls=%fused_computation.8 | convolution fusion | flops 2715321600 | bytes 6648844 | tf_op jit(solution)/shard_map/dot_general | solution.py:41
  286.5 0.0 copy-done.1
  286.5 61.6 %all-reduce.9 = bf16[1504,200]{0,1:T(8,128)(2,1)S(1)} all-reduce(f32[1504,200]{0,1:T(8,128)S(1)} %get-tuple-element.7), channel_id=1, replica_groups=mesh['gx'=8,'gy'=4] {'gx'}, use_global_device_ids=true, to_apply=%region_2.3 | all-reduce | flops 300800 | bytes 1804800 | tf_op jit(solution)/shard_map/psum | solution.py:50
  348.2 7.0 %convolution_bitcast_fusion = f32[2500,200]{0,1:T(8,128)} fusion(bf16[1504,2500]{0,1:T(8,128)(2,1)} %param.4, bf16[1504,200]{0,1:T(8,128)(2,1)S(1)} %all-reduce.9), kind=kOutput, calls=%fused_computation.3 | convolution fusion | flops 1504000000 | bytes 10121600 | tf_op jit(solution)/shard_map/dot_general | solution.py:52
  355.2 0.0 copy-start.2
  355.2 34.9 %fusion = f32[2500,56]{0,1:T(8,128)S(1)} fusion(f32[2500,200]{0,1:T(8,128)} %convolution_bitcast_fusion), kind=kCustom, calls=%all-reduce-scatter | all-reduce-scatter fusion | flops 560001 | bytes 2560512
  390.1 1.3 collective-permute-start
  391.4 0.0 copy-done.2
  391.4 0.6 dynamic-slice.5
  392.7 40.6 %all-reduce.2 = (f32[]{:T(128)}, f32[]{:T(128)}) all-reduce(f32[]{:T(128)} %get-tuple-element.6, f32[]{:T(128)} %get-tuple-element.8), channel_id=1, replica_groups=mesh['gx'=8,'gy'=4] {'gx','gy'}, use_global_device_ids=true, to_apply=%region_5.6 | all-reduce | flops 2 | bytes 16 | tf_op jit(solution)/shard_map/psum | solution.py:49
  434.5 0.0 collective-permute-done
  434.5 0.4 concatenate
  435.0 0.9 constant_dynamic-slice_fusion
  (3 shorter events, 0.0 us)
Async XLA Ops:
  7.2 1.2 copy-start
  7.2 103.4 %all-gather.6.cloned.1.call-start = ((), (), s32[]{:S(2)}) async-start(), calls=%async_computation.1 | async-start | bytes 3072000 | tf_op jit(solution)/shard_map/all_gather | solution.py:16
  74.2 137.1 %all-gather.8.cloned.1.call-start = ((), (), s32[]{:S(2)}) async-start(), calls=%async_computation.2 | async-start | bytes 5529600 | tf_op jit(solution)/shard_map/all_gather | solution.py:24
  131.3 142.1 %all-reduce.7.cloned.1.call-start = ((), (), s32[]{:S(2)}) async-start(), calls=%async_computation | async-start | bytes 4915200 | tf_op jit(solution)/shard_map/psum | solution.py:9
  281.5 5.0 %copy-start.1 = (f32[752,1504]{1,0:T(8,128)}, f32[752,1504]{1,0:T(8,128)S(1)}, u32[]{:S(2)}) copy-start(f32[752,1504]{1,0:T(8,128)S(1)} %get-tuple-element.9) | copy-start | bytes 13572100
  355.2 36.3 %copy-start.2 = (u32[32]{0:T(128)S(1)}, u32[32]{0:T(128)}, u32[]{:S(2)}) copy-start(u32[32]{0:T(128)} %constant.44) | copy-start | bytes 388
  390.1 44.4 %collective-permute-start = (f32[2500,18]{0,1:T(8,128)S(1)}, f32[2500,18]{0,1:T(8,128)S(1)}, u32[]{:S(2)}, u32[]{:S(2)}) collective-permute-start(f32[2500,18]{0,1:T(8,128)S(1)} %slice), channel_id=1, source_target_pairs={{0,1},{1,2},{2,3},{4,5},{5,6},{6,7},{8,9},{9,10},{10,11},{12,13},{... | collective-permute-start | bytes 540008
Sparse Core Ops, SparseCore 0:
  74.3 36.1 all-gather.5
  131.4 79.9 all-gather.7
  216.3 56.9 all-reduce.6
where the time goes:
time: 448 us; the launch traced here: 445 us
  blocking collectives  198 us (44%)
  waiting for transfers between devices  173 us (39%)
  matrix products  38.4 us (9%)
  between operations  18.1 us (4%)
  local copies, waits for them, and re-layouts  10.4 us (2%)
  other arithmetic  4.83 us (1%)
    all_gather x1, waiting for transfers between devices, on_device(): all_half = lax.all_gather(half, 'gx', axis=0, tiled=True)  79.8 us
    psum x1, blocking collectives, on_device(): applied = lax.psum(applied_part, 'gx')  61.6 us
    psum x1, blocking collectives, on_device(): own_admm = lax.psum(partial_value, 'gx').astype(jnp.bfloat16)  60.9 us
    psum x1, waiting for transfers between devices, spread(): return lax.psum(block, axis)  57.1 us
    psum x1, blocking collectives, on_device(): energy_total = lax.psum(energy_part, ('gx', 'gy'))  40.6 us
    all_gather x1, waiting for transfers between devices, on_device(): admm = lax.all_gather(own_admm, 'gy', axis=0, tiled=True)  36.3 us
    unnamed x1, blocking collectives  34.9 us
    dot_general x1, matrix products, on_device(): lax.dot_general(integrals, admm, (((2,), (0,)), ((), ())), preferred_elem...  13.3 us
  transfers between devices with their start and end apart: 4, of which 3 were waited for; matrix products, arithmetic and copies ran while one was open for 0% of the time, Pallas kernels for 0%

commit v1 on v0

v1 whole, which is shorter than its diff:
```python
import functools

import jax
import jax.numpy as jnp
from jax import lax
from jax.experimental import pallas as pl
from jax.experimental.pallas import tpu as pltpu
from jax.sharding import PartitionSpec as P

MESH = pl.DeviceIdType.MESH
LIMIT = 60 * 1024 * 1024


def factor(size):
    inner = 1
    while inner * inner * 4 <= size:
        inner *= 2
    return size // inner, inner


def up(value, unit):
    return -(-value // unit) * unit


def remote(src, dst, send, recv, dev):
    return pltpu.make_async_remote_copy(
        src_ref=src, dst_ref=dst, send_sem=send, recv_sem=recv, device_id=dev, device_id_type=MESH
    )


def greet(size_x, size_y):
    gx, gy = lax.axis_index("gx"), lax.axis_index("gy")
    barrier = pltpu.get_barrier_semaphore()

    def hello(step, carry):
        other = lax.rem(gx * size_y + gy + step, size_x * size_y)
        pl.semaphore_signal(
            barrier, inc=1, device_id=(other // size_y, lax.rem(other, size_y)), device_id_type=MESH
        )
        return carry

    lax.fori_loop(1, size_x * size_y, hello, 0)
    pl.semaphore_wait(barrier, size_x * size_y - 1)


def reduce_gather_kernel(
    size_x, size_y, wide, part, out, landing, send_a, recv_a, send_z, recv_z, send_x, recv_x, send_y, recv_y, send_c, recv_c
):
    gx, gy = lax.axis_index("gx"), lax.axis_index("gy")
    num_z, num_x = factor(size_x)
    z, x = gx // num_x, lax.rem(gx, num_x)
    num_y = size_y // 2
    y, c = gy // 2, lax.rem(gy, 2)
    greet(size_x, size_y)
    outgoing = []
    for d in range(1, size_x):
        to = lax.rem(gx + d, size_x)
        copy = remote(part.at[to], landing.at[d], send_a.at[d], recv_a.at[d], (to, gy))
        copy.start()
        outgoing.append(copy)
    total = part[gx].astype(jnp.float32)
    for d in range(1, size_x):
        outgoing[d - 1].wait_recv()
        total = total + landing[d].astype(jnp.float32)
    row = gy if wide else 0
    out[row, gx] = total.astype(out.dtype)
    pending = []

    def piece(group, who):
        return out.at[group, who]

    def to_core(group, who, slot):
        if wide:
            copy = remote(piece(group, who), piece(group, who), send_c.at[slot], recv_c.at[slot], (gx, gy + 1 - 2 * c))
            copy.start()
            pending.append(copy)

    def to_y(group, who, slot):
        if wide:
            for d in range(1, num_y):
                there = lax.rem(y + d, num_y)
                copy = remote(
                    piece(group, who), piece(group, who), send_y.at[slot, d], recv_y.at[slot, d], (gx, there * 2 + c)
                )
                copy.start()
                pending.append(copy)

    for d in range(1, num_z):
        to = lax.rem(z + d, num_z) * num_x + x
        copy = remote(piece(row, gx), piece(row, gx), send_z.at[d], recv_z.at[d], (to, gy))
        copy.start()
        pending.append(copy)
    for d in range(num_z):
        src_z = lax.rem(z - d + num_z, num_z)
        who = src_z * num_x + x
        if d > 0:
            remote(piece(row, who), piece(row, who), send_z.at[d], recv_z.at[d], (gx, gy)).wait_recv()
        for e in range(1, num_x):
            to = z * num_x + lax.rem(x + e, num_x)
            copy = remote(piece(row, who), piece(row, who), send_x.at[d, e], recv_x.at[d, e], (to, gy))
            copy.start()
            pending.append(copy)
        to_y(row, who, d * num_x)
        to_core(row, who, d * num_x)
    for d in range(num_z):
        src_z = lax.rem(z - d + num_z, num_z)
        for e in range(1, num_x):
            who = src_z * num_x + lax.rem(x - e + num_x, num_x)
            remote(piece(row, who), piece(row, who), send_x.at[d, e], recv_x.at[d, e], (gx, gy)).wait_recv()
            to_y(row, who, d * num_x + e)
            to_core(row, who, d * num_x + e)
    if wide:
        for d in range(num_z):
            for e in range(num_x):
                who = lax.rem(z - d + num_z, num_z) * num_x + lax.rem(x - e + num_x, num_x)
                slot = d * num_x + e
                for f in range(1, num_y):
                    group = lax.rem(y - f + num_y, num_y) * 2 + c
                    remote(piece(group, who), piece(group, who), send_y.at[slot, f], recv_y.at[slot, f], (gx, gy)).wait_recv()
                    to_core(group, who, f * size_x + slot)
        for d in range(num_z):
            for e in range(num_x):
                who = lax.rem(z - d + num_z, num_z) * num_x + lax.rem(x - e + num_x, num_x)
                for f in range(num_y):
                    group = lax.rem(y - f + num_y, num_y) * 2 + 1 - c
                    slot = f * size_x + d * num_x + e
                    remote(piece(group, who), piece(group, who), send_c.at[slot], recv_c.at[slot], (gx, gy)).wait_recv()
    for copy in outgoing:
        copy.wait_send()
    for copy in pending:
        copy.wait_send()


def reduce_gather(part, size_x, size_y, wide, number):
    rows, cols = part.shape
    chunk = up(-(-rows // size_x), 16)
    padded = jnp.pad(part.astype(jnp.bfloat16), ((0, chunk * size_x - rows), (0, 0)))
    padded = padded.reshape(size_x, chunk, cols)
    num_z, num_x = factor(size_x)
    groups = size_y if wide else 1
    dma = pltpu.SemaphoreType.DMA
    out = pl.pallas_call(
        functools.partial(reduce_gather_kernel, size_x, size_y, wide),
        out_shape=jax.ShapeDtypeStruct((groups, size_x, chunk, cols), jnp.bfloat16),
        in_specs=[pl.BlockSpec(memory_space=pltpu.VMEM)],
        out_specs=pl.BlockSpec(memory_space=pltpu.VMEM),
        scratch_shapes=[
            pltpu.VMEM((size_x, chunk, cols), jnp.bfloat16),
            dma((size_x,)),
            dma((size_x,)),
            dma((num_z,)),
            dma((num_z,)),
            dma((num_z, num_x)),
            dma((num_z, num_x)),
            dma((size_x, size_y // 2)),
            dma((size_x, size_y // 2)),
            dma((size_x * size_y // 2,)),
            dma((size_x * size_y // 2,)),
        ],
        compiler_params=pltpu.CompilerParams(collective_id=number, has_side_effects=True, vmem_limit_bytes=LIMIT),
    )(padded)
    return out.reshape(groups, size_x * chunk, cols)[:, :rows]


def exchange_kernel(
    size_x, size_y, block, own, out, cols, rows, acc, own_sem, send_u, recv_u, send_d, recv_d, send_x, recv_x, send_y, recv_y, send_c, recv_c, row_sem
):
    gx, gy = lax.axis_index("gx"), lax.axis_index("gy")
    num_z, num_x = factor(size_x)
    z, x = gx // num_x, lax.rem(gx, num_x)
    num_y = size_y // 2
    y, c = gy // 2, lax.rem(gy, 2)
    width = out.shape[1]
    window = rows.shape[2]
    per = size_x // size_y
    root = gx // per
    root_y, root_c = root // 2, lax.rem(root, 2)
    offset = lax.rem(gx, per) * block
    first = pl.multiple_of(jnp.minimum(offset // 128 * 128, cols.shape[2] - window), 128)
    mine = gy == root
    below = (y != root_y) & (c == root_c)
    last = c != root_c
    greet(size_x, size_y)
    mypiece = pltpu.make_async_copy(own, cols.at[gx], own_sem)
    mypiece.start()
    mypiece.wait()

    def upward(k):
        who = jnp.maximum(z - k, 0) * num_x + x
        return remote(cols.at[who], cols.at[who], send_u.at[k], recv_u.at[k], (jnp.minimum(z + 1, num_z - 1) * num_x + x, gy))

    def downward(k):
        who = jnp.minimum(z + k, num_z - 1) * num_x + x
        return remote(cols.at[who], cols.at[who], send_d.at[k], recv_d.at[k], (jnp.maximum(z - 1, 0) * num_x + x, gy))

    def sideways(slot, who, e):
        to = z * num_x + lax.rem(x + e, num_x)
        return remote(cols.at[who], cols.at[who], send_x.at[slot, e], recv_x.at[slot, e], (to, gy))

    def row_y(who, f):
        return remote(
            cols.at[who, :, pl.ds(first, window)], rows.at[who], send_y.at[who, f], recv_y.at[who], (gx, lax.rem(y + f, num_y) * 2 + c)
        )

    def row_c(who, source):
        return remote(source, rows.at[who], send_c.at[who], recv_c.at[who], (gx, gy + 1 - 2 * c))

    def row_own(who):
        return pltpu.make_async_copy(cols.at[who, :, pl.ds(first, window)], rows.at[who], row_sem.at[who])

    def have(who):
        @pl.when(mine)
        def _():
            for f in range(1, num_y):
                row_y(who, f).start()
            row_c(who, cols.at[who, :, pl.ds(first, window)]).start()
            row_own(who).start()

    def spread(slot, who):
        for e in range(1, num_x):
            sideways(slot, who, e).start()
        have(who)

    for k in range(num_z):
        if k > 0:
            @pl.when(z >= k)
            def _(k=k):
                who = jnp.maximum(z - k, 0) * num_x + x
                remote(cols.at[who], cols.at[who], send_u.at[k - 1], recv_u.at[k - 1], (gx, gy)).wait_recv()
        if k < num_z - 1:
            @pl.when((z >= k) & (z < num_z - 1))
            def _(k=k):
                upward(k).start()
        if k > 0:
            @pl.when(z + k < num_z)
            def _(k=k):
                who = jnp.minimum(z + k, num_z - 1) * num_x + x
                remote(cols.at[who], cols.at[who], send_d.at[k - 1], recv_d.at[k - 1], (gx, gy)).wait_recv()
        if k < num_z - 1:
            @pl.when((z + k < num_z) & (z > 0))
            def _(k=k):
                downward(k).start()
        for side in ((1, -1) if k else (1,)):
            src_z = z - side * k
            @pl.when((src_z >= 0) & (src_z < num_z))
            def _(src_z=src_z):
                src_z = jnp.clip(src_z, 0, num_z - 1)
                spread(src_z, src_z * num_x + x)
        for side in ((1, -1) if k else (1,)):
            src_z = z - side * k
            @pl.when((src_z >= 0) & (src_z < num_z))
            def _(src_z=src_z):
                src_z = jnp.clip(src_z, 0, num_z - 1)
                for e in range(1, num_x):
                    who = src_z * num_x + lax.rem(x - e + num_x, num_x)
                    sideways(src_z, who, e).wait_recv()
                    have(who)

    def finish(who, carry):
        @pl.when(mine)
        def _():
            row_own(who).wait()

        @pl.when(below)
        def _():
            row_y(who, 1).wait_recv()
            row_c(who, rows.at[who]).start()

        @pl.when(last)
        def _():
            row_c(who, rows.at[who]).wait_recv()

        for start in range(0, width, 512):
            span = min(512, width - start)
            term = lax.dot_general(
                rows[who], cols[who, :, start:start + span], (((0,), (0,)), ((), ())), preferred_element_type=jnp.float32
            )

            @pl.when(who == 0)
            def _():
                acc[:, start:start + span] = term

            @pl.when(who > 0)
            def _():
                acc[:, start:start + span] += term
        return carry

    lax.fori_loop(0, size_x, finish, 0)
    for i in range(per):
        at = i * block - min(i * block // 128 * 128, cols.shape[2] - window)

        @pl.when(lax.rem(gx, per) == i)
        def _(at=at):
            out[...] = acc[at:at + block, :]

    for k in range(num_z - 1):
        @pl.when((z >= k) & (z < num_z - 1))
        def _(k=k):
            upward(k).wait_send()

        @pl.when((z + k < num_z) & (z > 0))
        def _(k=k):
            downward(k).wait_send()
    for src_z in range(num_z):
        for e in range(1, num_x):
            sideways(src_z, src_z * num_x + x, e).wait_send()

    def drain(who, carry):
        @pl.when(mine)
        def _():
            for f in range(1, num_y):
                row_y(who, f).wait_send()

        @pl.when(mine | below)
        def _():
            row_c(who, rows.at[who]).wait_send()

        return carry

    lax.fori_loop(0, size_x, drain, 0)


def exchange_of(half_t, size_x, size_y, block, number):
    occ, width = half_t.shape
    num_z, num_x = factor(size_x)
    per = size_x // size_y
    padded = up(width, 128)
    window = max(up(i * block % 128 + block, 128) for i in range(per))
    dma = pltpu.SemaphoreType.DMA
    half_t = jnp.pad(half_t, ((0, 0), (0, padded - width)))
    return pl.pallas_call(
        functools.partial(exchange_kernel, size_x, size_y, block),
        out_shape=jax.ShapeDtypeStruct((block, width), jnp.float32),
        in_specs=[pl.BlockSpec(memory_space=pltpu.VMEM)],
        out_specs=pl.BlockSpec(memory_space=pltpu.VMEM),
        scratch_shapes=[
            pltpu.VMEM((size_x, occ, padded), jnp.bfloat16),
            pltpu.VMEM((size_x, occ, window), jnp.bfloat16),
            pltpu.VMEM((window, width), jnp.float32),
            dma(()),
            dma((num_z,)),
            dma((num_z,)),
            dma((num_z,)),
            dma((num_z,)),
            dma((num_z, num_x)),
            dma((num_z, num_x)),
            dma((size_x, size_y // 2)),
            dma((size_x,)),
            dma((size_x,)),
            dma((size_x,)),
            dma((size_x,)),
        ],
        compiler_params=pltpu.CompilerParams(collective_id=number, has_side_effects=True, vmem_limit_bytes=LIMIT),
    )(half_t)


def on_device(size_x, size_y, orbitals, projector, integrals):
    part_rows = projector.shape[0]
    partial_value = jnp.dot(projector, orbitals, preferred_element_type=jnp.float32)
    groups = reduce_gather(partial_value, size_x, size_y, True, 1)
    occ = groups.shape[2]
    total_adm = part_rows * size_y
    admm = groups.reshape(total_adm, occ)
    half_t = lax.dot_general(
        admm, integrals[0], (((0,), (1,)), ((), ())), preferred_element_type=jnp.float32
    ).astype(jnp.bfloat16)
    exchange = exchange_of(half_t, size_x, size_y, total_adm // size_x, 2)
    own = lax.dynamic_index_in_dim(groups, lax.axis_index("gy"), 0, keepdims=False)
    mixed = lax.psum(jnp.dot(half_t, own, preferred_element_type=jnp.float32), "gy")
    wide = half_t.astype(jnp.float32)
    trace_part = jnp.sum(wide * wide)
    energy_part = jnp.sum(mixed * mixed) / size_y
    energy_total, trace_total = lax.psum((energy_part, trace_part), ("gx", "gy"))
    applied_part = lax.dot_general(
        half_t, mixed.astype(jnp.bfloat16), (((0,), (0,)), ((), ())), preferred_element_type=jnp.float32
    )
    applied_low = reduce_gather(applied_part, size_x, size_y, False, 3)[0]
    back_part = lax.dot_general(
        projector, applied_low, (((0,), (0,)), ((), ())), preferred_element_type=jnp.float32
    )
    back = lax.psum_scatter(back_part, "gy", scatter_dimension=1, tiled=True)
    energy_mean = -0.5 * energy_total / (total_adm * occ)
    trace_mean = trace_total / total_adm
    return (exchange, back, energy_mean, trace_mean)


def solution(mesh):
    return jax.shard_map(
        functools.partial(on_device, mesh.shape["gx"], mesh.shape["gy"]),
        mesh=mesh,
        in_specs=(P("gx", None), P("gy", "gx"), P("gx", "gy", None)),
        out_specs=(P("gx", "gy"), P("gx", "gy"), P(), P()),
        check_vma=False,
    )
```

time: 448 us -> 352 us (0.79)
  Pallas kernels: 0 us -> 188 us
  waiting for transfers between devices: 173 us -> 28.9 us
  blocking collectives: 198 us -> 66.5 us
  matrix products: 38.4 us -> 28.6 us
  local copies, waits for them, and re-layouts: 10.4 us -> 15 us
    pallas_call x0 -> x3, Pallas kernels: none -> 188 us  [the longest x1 97.3 us: exchange_of(): pl.pallas_call(functools.partial(exchange_kernel, size_x, size_y, block),...]
    psum x3 -> x1, blocking collectives: 163 us -> 39.9 us  [on_device(): lax.psum((energy_part, trace_part), ('gx', 'gy'))]
    all_gather x2 -> x0, waiting for transfers between devices: 116 us -> none  [the longest x1 79.8 us: on_device(): all_half = lax.all_gather(half, 'gx', axis=0, tiled=True)]
    psum x1, waiting for transfers between devices: 57.1 us -> 28.8 us  [on_device(): lax.psum(jnp.dot(half_t, own, preferred_element_type=jnp.float32), 'gy')]
    dot_general x3, matrix products: 26.5 us -> 16.4 us  [the longest x1 12.9 us: on_device(): lax.dot_general(admm, integrals[0], (((0,), (1,)), ((), ())), preferred_e...]
    unnamed x1, blocking collectives: 34.9 us -> 26.6 us
    select_n x1 -> x0, other arithmetic: 4.82 us -> none  [spread(): jnp.where(lax.axis_index(axis) == holder, block, jnp.zeros_like(block))]
  transfers between devices with their start and end apart: 4 -> 2, of which waited for: 3 -> 1; matrix products, arithmetic and copies ran while one was open for 0% -> 1% of each run, Pallas kernels for 0% -> 28%
where the time goes in v1:
time: 352 us; the launch traced here: 348 us
  Pallas kernels  188 us (53%)
  blocking collectives  66.5 us (19%)
  waiting for transfers between devices  28.9 us (8%)
  matrix products  28.6 us (8%)
  between operations  19 us (5%)
  local copies, waits for them, and re-layouts  15 us (4%)
    pallas_call x1, Pallas kernels, exchange_of(): pl.pallas_call(functools.partial(exchange_kernel, size_x, size_y, block),...  97.3 us
    pallas_call x2, Pallas kernels, reduce_gather(): pl.pallas_call(functools.partial(reduce_gather_kernel, size_x, size_y, wi...  91.1 us
    psum x1, blocking collectives, on_device(): lax.psum((energy_part, trace_part), ('gx', 'gy'))  39.9 us
    psum x1, waiting for transfers between devices, on_device(): lax.psum(jnp.dot(half_t, own, preferred_element_type=jnp.float32), 'gy')  28.8 us
    unnamed x1, blocking collectives  26.6 us
    dot_general x1, matrix products, on_device(): lax.dot_general(admm, integrals[0], (((0,), (1,)), ((), ())), preferred_e...  12.9 us
    unnamed x13, local copies, waits for them, and re-layouts  8.39 us
    dot_general x1, matrix products, on_device(): lax.dot_general(projector, applied_low, (((0,), (0,)), ((), ())), preferr...  7.3 us
  transfers between devices with their start and end apart: 2, of which 1 were waited for; matrix products, arithmetic and copies ran while one was open for 1% of the time, Pallas kernels for 28%

profile of v1, /device:TPU:7, one launch (start us, length us, event | category | flops | bytes accessed | tf_op | source)
XLA Modules:
  0.0 348.4 jit_solution(1409778481344567320)
XLA Ops:
  7.2 0.0 copy-start
  7.2 0.0 all-reduce.8.cloned.1.call-start
  7.2 1.2 copy-done
  8.4 4.9 %convolution_convert_fusion = bf16[1504,200]{0,1:T(8,128)(2,1)S(1)} fusion(bf16[1504,2500]{0,1:T(8,128)(2,1)} %param.4, bf16[2500,200]{0,1:T(8,128)(2,1)S(1)} %copy-done), kind=kOutput, calls=%fused_computation.3 | convolution fusion | flops 1504300800 | bytes 9121600 | tf_op jit(solution)/shard_map/dot_general | solution.py:359
  13.3 0.3 copy.11
  13.6 1.0 pad.11.clone
  14.6 53.1 %shard_map.66 = bf16[4,8,192,200]{3,2,1,0:T(8,128)(2,1)} custom-call(bf16[8,192,200]{2,1,0:T(8,128)(2,1)} %bitcast.32), custom_call_target="tpu_custom_call" | custom-call | tf_op jit(solution)/shard_map/pallas_call | solution.py:142
  67.7 3.7 %slice.8 = bf16[4,1504,200]{2,1,0:T(8,128)(2,1)} slice(bf16[4,1536,200]{2,1,0:T(8,128)(2,1)} %bitcast.29), slice={[0:4], [0:1504], [0:200]} | slice | bytes 4812800 | tf_op jit(solution)/shard_map/slice | solution.py:162
  71.5 12.9 %multiply_reduce_fusion = (f32[]{:T(128)}, bf16[200,1504]{1,0:T(8,128)(2,1)S(1)}) fusion(bf16[6016,200]{1,0:T(8,128)(2,1)} %bitcast.30, bf16[1,1504,6016]{2,1,0:T(8,128)(2,1)} %param.5), kind=kOutput, calls=%fused_computation.6 | convolution fusion | flops 3620428800 | bytes 21104132 | tf_op jit(solution)/shard_map/dot_general | solution.py:364
  84.4 2.1 fusion.6
  86.5 0.0 all-reduce.8.cloned.1.call-update
  86.6 28.8 %all-reduce.8.cloned.1.call-done = f32[200,200]{1,0:T(8,128)} async-done(((f32[200,200]{1,0:T(8,128)}), f32[200,200]{1,0:T(8,128)}) %all-reduce.8.cloned.1.call-update) | async-done | bytes 160016 | tf_op jit(solution)/shard_map/psum | solution.py:369
  115.4 1.3 convolution_convert_fusion.1
  116.7 0.3 copy.12
  117.0 1.0 pad.13.clone
  118.0 38.0 %shard_map.68 = bf16[1,8,192,200]{3,2,1,0:T(8,128)(2,1)} custom-call(bf16[8,192,200]{2,1,0:T(8,128)(2,1)} %bitcast.31), custom_call_target="tpu_custom_call" | custom-call | tf_op jit(solution)/shard_map/pallas_call | solution.py:142
  156.0 7.3 %convolution_bitcast_fusion = f32[2500,200]{0,1:T(8,128)} fusion(bf16[1504,2500]{0,1:T(8,128)(2,1)} %param.4, bf16[1,1536,200]{2,1,0:T(8,128)(2,1)} %bitcast.33), kind=kOutput, calls=%fused_computation.2 | convolution fusion | flops 1504000000 | bytes 10462336 | tf_op jit(solution)/shard_map/dot_general | solution.py:378
  163.3 26.6 %fusion = f32[2500,56]{0,1:T(8,128)S(1)} fusion(f32[2500,200]{0,1:T(8,128)} %convolution_bitcast_fusion), kind=kCustom, calls=%all-reduce-scatter | all-reduce-scatter fusion | flops 560001 | bytes 2560512
  189.9 1.3 collective-permute-start
  191.2 0.0 copy-start.2
  191.2 0.0 copy-start.1
  191.2 0.9 pad.12.own
  192.1 97.3 %shard_map.67 = f32[752,1504]{1,0:T(8,128)} custom-call(bf16[200,1536]{1,0:T(8,128)(2,1)} %pad.12.own), custom_call_target="tpu_custom_call" | custom-call | tf_op jit(solution)/shard_map/pallas_call | solution.py:331
  289.4 0.0 copy-done.2
  289.4 0.6 dynamic-slice.4
  290.6 0.0 copy-done.1
  290.7 0.7 multiply_reduce_fusion.1
  292.0 39.9 %all-reduce.5 = (f32[]{:T(128)}, f32[]{:T(128)}) all-reduce(f32[]{:T(128)S(6)} %div.9, f32[]{:T(128)} %get-tuple-element.6), channel_id=1, replica_groups=mesh['gx'=8,'gy'=4] {'gx','gy'}, use_global_device_ids=true, to_apply=%region_3.4 | all-reduce | flops 2 | bytes 16 | tf_op jit(solution)/shard_map/psum | solution.py:373
  333.2 0.0 collective-permute-done
  333.2 0.4 concatenate
  333.6 0.9 constant_dynamic-slice_fusion
  334.5 4.8 %copy.15 = f32[752,1504]{1,0:T(8,128)} copy(f32[752,1504]{1,0:T(8,128)} %shard_map.67) | data formatting | bytes 9048064
  (1 shorter events, 0.0 us)
Async XLA Ops:
  7.2 1.2 copy-start
  7.2 108.2 %all-reduce.8.cloned.1.call-start = ((), (), s32[]{:S(2)}) async-start(), calls=%async_computation | async-start | bytes 409600 | tf_op jit(solution)/shard_map/psum | solution.py:369
  189.9 143.3 %collective-permute-start = (f32[2500,18]{0,1:T(8,128)S(1)}, f32[2500,18]{0,1:T(8,128)S(1)}, u32[]{:S(2)}, u32[]{:S(2)}) collective-permute-start(f32[2500,18]{0,1:T(8,128)S(1)} %slice.10), channel_id=1, source_target_pairs={{0,1},{1,2},{2,3},{4,5},{5,6},{6,7},{8,9},{9,10},{10,11},{12,13},{... | collective-permute-start | bytes 540008
  191.2 98.2 %copy-start.2 = (u32[32]{0:T(128)S(1)}, u32[32]{0:T(128)}, u32[]{:S(2)}) copy-start(u32[32]{0:T(128)} %constant.37) | copy-start | bytes 388
  191.2 99.4 %copy-start.1 = (f32[200,200]{1,0:T(8,128)S(1)}, f32[200,200]{1,0:T(8,128)}, u32[]{:S(2)}) copy-start(f32[200,200]{1,0:T(8,128)} %all-reduce.8.cloned.1.call-done) | copy-start | bytes 480004
Sparse Core Ops, SparseCore 0:
  86.7 28.6 all-reduce.7

commit v2 on v1

--- a/solution.py
+++ b/solution.py
@@ -163,7 +163,7 @@
 
 
 def exchange_kernel(
-    size_x, size_y, block, own, out, cols, rows, acc, own_sem, send_u, recv_u, send_d, recv_d, send_x, recv_x, send_y, recv_y, send_c, recv_c, row_sem
+    size_x, size_y, block, own, stats, out, sums, cols, rows, acc, landing, send_s, recv_s, own_sem, send_u, recv_u, send_d, recv_d, send_x, recv_x, send_y, recv_y, send_c, recv_c, row_sem
 ):
     gx, gy = lax.axis_index("gx"), lax.axis_index("gy")
     num_z, num_x = factor(size_x)
@@ -184,6 +184,11 @@
     mypiece = pltpu.make_async_copy(own, cols.at[gx], own_sem)
     mypiece.start()
     mypiece.wait()
+    devices = size_x * size_y
+    me = gx * size_y + gy
+
+    def stat_copy(slot, step, to):
+        return remote(stats, landing.at[slot], send_s.at[step], recv_s.at[slot], (to // size_y, lax.rem(to, size_y)))
 
     def upward(k):
         who = jnp.maximum(z - k, 0) * num_x + x
@@ -220,6 +225,45 @@
         for e in range(1, num_x):
             sideways(slot, who, e).start()
         have(who)
+
+    def add_term(who, fresh):
+        @pl.when(mine)
+        def _():
+            row_own(who).wait()
+
+        @pl.when(below)
+        def _():
+            row_y(who, 1).wait_recv()
+            row_c(who, rows.at[who]).start()
+
+        @pl.when(last)
+        def _():
+            row_c(who, rows.at[who]).wait_recv()
+
+        for start in range(0, width, 512):
+            span = min(512, width - start)
+            term = lax.dot_general(
+                rows[who], cols[who, :, start:start + span], (((0,), (0,)), ((), ())), preferred_element_type=jnp.float32
+            )
+            if fresh:
+                acc[:, start:start + span] = term
+            else:
+                acc[:, start:start + span] += term
+
+    def add_terms(k):
+        if k == 0:
+            add_term(gx, True)
+
+        def one(i, carry):
+            src_z = z + jnp.where(i < num_x, -k, k)
+
+            @pl.when((src_z >= 0) & (src_z < num_z))
+            def _():
+                add_term(src_z * num_x + lax.rem(x + lax.rem(i, num_x), num_x), False)
+
+            return carry
+
+        lax.fori_loop(0 if k else 1, 2 * num_x if k else num_x, one, 0)
 
     for k in range(num_z):
         if k > 0:
@@ -246,6 +290,14 @@
             def _(src_z=src_z):
                 src_z = jnp.clip(src_z, 0, num_z - 1)
                 spread(src_z, src_z * num_x + x)
+        if k == 0:
+            def tell(step, carry):
+                stat_copy(me, step, lax.rem(me + step, devices)).start()
+                return carry
+
+            lax.fori_loop(1, devices, tell, 0)
+        else:
+            add_terms(k - 1)
         for side in ((1, -1) if k else (1,)):
             src_z = z - side * k
             @pl.when((src_z >= 0) & (src_z < num_z))
@@ -255,37 +307,21 @@
                     who = src_z * num_x + lax.rem(x - e + num_x, num_x)
                     sideways(src_z, who, e).wait_recv()
                     have(who)
-
-    def finish(who, carry):
-        @pl.when(mine)
-        def _():
-            row_own(who).wait()
-
-        @pl.when(below)
-        def _():
-            row_y(who, 1).wait_recv()
-            row_c(who, rows.at[who]).start()
-
-        @pl.when(last)
-        def _():
-            row_c(who, rows.at[who]).wait_recv()
-
-        for start in range(0, width, 512):
-            span = min(512, width - start)
-            term = lax.dot_general(
-                rows[who], cols[who, :, start:start + span], (((0,), (0,)), ((), ())), preferred_element_type=jnp.float32
-            )
-
-            @pl.when(who == 0)
-            def _():
-                acc[:, start:start + span] = term
-
-            @pl.when(who > 0)
-            def _():
-                acc[:, start:start + span] += term
+    add_terms(num_z - 1)
+
+    def hear(step, carry):
+        stat_copy(lax.rem(me + step, devices), step, me).wait_recv()
         return carry
 
-    lax.fori_loop(0, size_x, finish, 0)
+    lax.fori_loop(1, devices, hear, 0)
+    landing[me] = stats[...]
+    sums[...] = jnp.sum(landing[...], axis=0)
+
+    def told(step, carry):
+        stat_copy(me, step, me).wait_send()
+        return carry
+
+    lax.fori_loop(1, devices, told, 0)
     for i in range(per):
         at = i * block - min(i * block // 128 * 128, cols.shape[2] - window)
 
@@ -320,7 +356,7 @@
     lax.fori_loop(0, size_x, drain, 0)
 
 
-def exchange_of(half_t, size_x, size_y, block, number):
+def exchange_of(half_t, stats, size_x, size_y, block, number):
     occ, width = half_t.shape
     num_z, num_x = factor(size_x)
     per = size_x // size_y
@@ -330,13 +366,16 @@
     half_t = jnp.pad(half_t, ((0, 0), (0, padded - width)))
     return pl.pallas_call(
         functools.partial(exchange_kernel, size_x, size_y, block),
-        out_shape=jax.ShapeDtypeStruct((block, width), jnp.float32),
-        in_specs=[pl.BlockSpec(memory_space=pltpu.VMEM)],
-        out_specs=pl.BlockSpec(memory_space=pltpu.VMEM),
+        out_shape=(jax.ShapeDtypeStruct((block, width), jnp.float32), jax.ShapeDtypeStruct(stats.shape, jnp.float32)),
+        in_specs=[pl.BlockSpec(memory_space=pltpu.VMEM)] * 2,
+        out_specs=[pl.BlockSpec(memory_space=pltpu.VMEM)] * 2,
         scratch_shapes=[
             pltpu.VMEM((size_x, occ, padded), jnp.bfloat16),
             pltpu.VMEM((size_x, occ, window), jnp.bfloat16),
             pltpu.VMEM((window, width), jnp.float32),
+            pltpu.VMEM((size_x * size_y,) + stats.shape, jnp.float32),
+            dma((size_x * size_y,)),
+            dma((size_x * size_y,)),
             dma(()),
             dma((num_z,)),
             dma((num_z,)),
@@ -351,7 +390,41 @@
             dma((size_x,)),
         ],
         compiler_params=pltpu.CompilerParams(collective_id=number, has_side_effects=True, vmem_limit_bytes=LIMIT),
-    )(half_t)
+    )(half_t, stats)
+
+
+def sum_kernel(size_y, same, part, out, landing, send, recv):
+    gx, gy = lax.axis_index("gx"), lax.axis_index("gy")
+    barrier = pltpu.get_barrier_semaphore()
+    for d in range(1, size_y):
+        pl.semaphore_signal(barrier, inc=1, device_id=(gx, lax.rem(gy + d, size_y)), device_id_type=MESH)
+    pl.semaphore_wait(barrier, size_y - 1)
+    copies = []
+    for d in range(1, size_y):
+        to = lax.rem(gy + d, size_y)
+        copy = remote(part.at[0 if same else to], landing.at[d], send.at[d], recv.at[d], (gx, to))
+        copy.start()
+        copies.append(copy)
+    total = part[0 if same else gy].astype(jnp.float32)
+    for d in range(1, size_y):
+        copies[d - 1].wait_recv()
+        total = total + landing[d].astype(jnp.float32)
+    out[...] = total
+    for copy in copies:
+        copy.wait_send()
+
+
+def sum_over_y(part, size_y, same, number):
+    shape = part.shape[1:]
+    dma = pltpu.SemaphoreType.DMA
+    return pl.pallas_call(
+        functools.partial(sum_kernel, size_y, same),
+        out_shape=jax.ShapeDtypeStruct(shape, jnp.float32),
+        in_specs=[pl.BlockSpec(memory_space=pltpu.VMEM)],
+        out_specs=pl.BlockSpec(memory_space=pltpu.VMEM),
+        scratch_shapes=[pltpu.VMEM((size_y,) + shape, part.dtype), dma((size_y,)), dma((size_y,))],
+        compiler_params=pltpu.CompilerParams(collective_id=number, has_side_effects=True, vmem_limit_bytes=LIMIT),
+    )(part)
 
 
 def on_device(size_x, size_y, orbitals, projector, integrals):
@@ -364,21 +437,24 @@
     half_t = lax.dot_general(
         admm, integrals[0], (((0,), (1,)), ((), ())), preferred_element_type=jnp.float32
     ).astype(jnp.bfloat16)
-    exchange = exchange_of(half_t, size_x, size_y, total_adm // size_x, 2)
     own = lax.dynamic_index_in_dim(groups, lax.axis_index("gy"), 0, keepdims=False)
-    mixed = lax.psum(jnp.dot(half_t, own, preferred_element_type=jnp.float32), "gy")
+    mixed_part = jnp.dot(half_t, own, preferred_element_type=jnp.float32)
+    mixed = sum_over_y(mixed_part[None], size_y, True, 4)
     wide = half_t.astype(jnp.float32)
     trace_part = jnp.sum(wide * wide)
     energy_part = jnp.sum(mixed * mixed) / size_y
-    energy_total, trace_total = lax.psum((energy_part, trace_part), ("gx", "gy"))
+    lane = lax.broadcasted_iota(jnp.int32, (8, 128), 1)
+    stats = jnp.where(lane == 0, energy_part, jnp.where(lane == 1, trace_part, 0.0))
     applied_part = lax.dot_general(
         half_t, mixed.astype(jnp.bfloat16), (((0,), (0,)), ((), ())), preferred_element_type=jnp.float32
     )
     applied_low = reduce_gather(applied_part, size_x, size_y, False, 3)[0]
     back_part = lax.dot_general(
-        projector, applied_low, (((0,), (0,)), ((), ())), preferred_element_type=jnp.float32
-    )
-    back = lax.psum_scatter(back_part, "gy", scatter_dimension=1, tiled=True)
+        applied_low, projector, (((0,), (0,)), ((), ())), preferred_element_type=jnp.float32
+    ).astype(jnp.bfloat16)
+    back = sum_over_y(back_part.reshape(size_y, occ // size_y, -1), size_y, False, 5).T
+    exchange, sums = exchange_of(half_t, stats, size_x, size_y, total_adm // size_x, 2)
+    energy_total, trace_total = sums[0, 0], sums[0, 1]
     energy_mean = -0.5 * energy_total / (total_adm * occ)
     trace_mean = trace_total / total_adm
     return (exchange, back, energy_mean, trace_mean)

time: 352 us -> 263 us (0.75)
  blocking collectives: 66.5 us -> 0 us
  waiting for transfers between devices: 28.9 us -> 0 us
  Pallas kernels: 188 us -> 211 us
  between operations: 19 us -> 4.95 us
    psum x1 -> x0, blocking collectives: 39.9 us -> none  [on_device(): lax.psum((energy_part, trace_part), ('gx', 'gy'))]
    pallas_call x0 -> x2, Pallas kernels: none -> 33.7 us  [sum_over_y(): pl.pallas_call(functools.partial(sum_kernel, size_y, same), out_shape=jax...]
    psum x1 -> x0, waiting for transfers between devices: 28.8 us -> none  [on_device(): lax.psum(jnp.dot(half_t, own, preferred_element_type=jnp.float32), 'gy')]
    unnamed x1 -> x0, blocking collectives: 26.6 us -> none
    pallas_call x1, Pallas kernels: 97.3 us -> 89.1 us  [exchange_of(): pl.pallas_call(functools.partial(exchange_kernel, size_x, size_y, block),...]
    unnamed x13 -> x8, local copies, waits for them, and re-layouts: 8.39 us -> 7.39 us
  transfers between devices with their start and end apart: 2 -> 0, of which waited for: 1 -> 0; matrix products, arithmetic and copies ran while one was open for 1% -> 0% of each run, Pallas kernels for 28% -> 0%
where the time goes in v2:
time: 263 us
  Pallas kernels  211 us (80%)
  matrix products  27.3 us (10%)
  local copies, waits for them, and re-layouts  16.7 us (6%)
  between operations  4.95 us (2%)
  other arithmetic  2.84 us (1%)
    pallas_call x1, Pallas kernels, exchange_of(): pl.pallas_call(functools.partial(exchange_kernel, size_x, size_y, block),...  89.1 us
    pallas_call x2, Pallas kernels, reduce_gather(): pl.pallas_call(functools.partial(reduce_gather_kernel, size_x, size_y, wi...  88.1 us
    pallas_call x2, Pallas kernels, sum_over_y(): pl.pallas_call(functools.partial(sum_kernel, size_y, same), out_shape=jax...  33.7 us
    dot_general x1, matrix products, on_device(): lax.dot_general(admm, integrals[0], (((0,), (1,)), ((), ())), preferred_e...  12.9 us
    unnamed x8, local copies, waits for them, and re-layouts  7.39 us
    dot_general x1, matrix products, on_device(): lax.dot_general(applied_low, projector, (((0,), (0,)), ((), ())), preferr...  6 us

profile of v2, /device:TPU:7, one launch (start us, length us, event | category | flops | bytes accessed | tf_op | source)
XLA Modules:
  0.0 262.7 jit_solution(12264888154988860980)
XLA Ops:
  0.6 0.0 copy-start
  0.7 1.2 copy-done
  1.9 4.9 %convolution_convert_fusion.1 = bf16[1504,200]{0,1:T(8,128)(2,1)S(1)} fusion(bf16[1504,2500]{0,1:T(8,128)(2,1)} %param.4, bf16[2500,200]{0,1:T(8,128)(2,1)S(1)} %copy-done), kind=kOutput, calls=%fused_computation.3 | convolution fusion | flops 1504300800 | bytes 9121600 | tf_op jit(solution)/shard_map/dot_general | solution.py:432
  6.8 0.3 copy.11
  7.1 1.0 pad.11.clone
  8.1 53.1 %shard_map.66 = bf16[4,8,192,200]{3,2,1,0:T(8,128)(2,1)} custom-call(bf16[8,192,200]{2,1,0:T(8,128)(2,1)} %bitcast.32), custom_call_target="tpu_custom_call" | custom-call | tf_op jit(solution)/shard_map/pallas_call | solution.py:142
  61.2 3.7 %slice.16 = bf16[4,1504,200]{2,1,0:T(8,128)(2,1)} slice(bf16[4,1536,200]{2,1,0:T(8,128)(2,1)} %bitcast.29), slice={[0:4], [0:1504], [0:200]} | slice | bytes 4812800 | tf_op jit(solution)/shard_map/slice | solution.py:162
  64.9 12.9 %multiply_reduce_fusion = (f32[]{:T(128)}, bf16[200,1504]{1,0:T(8,128)(2,1)S(1)}) fusion(bf16[6016,200]{1,0:T(8,128)(2,1)} %bitcast.30, bf16[1,1504,6016]{2,1,0:T(8,128)(2,1)} %param.5), kind=kOutput, calls=%fused_computation.6 | convolution fusion | flops 3620428800 | bytes 21104132 | tf_op jit(solution)/shard_map/dot_general | solution.py:437
  77.9 2.1 convolution_bitcast_fusion.part
  80.0 12.9 %shard_map.67 = f32[200,200]{1,0:T(8,128)} custom-call(f32[1,200,200]{2,1,0:T(8,128)} %convolution_bitcast_fusion.part), custom_call_target="tpu_custom_call" | custom-call | tf_op jit(solution)/shard_map/pallas_call | solution.py:420
  92.9 1.6 multiply_reduce_fusion.1
  95.1 0.7 compare_select_fusion
  95.8 0.6 broadcast_select_fusion.stats
  96.4 1.3 convolution_convert_fusion.2
  97.7 0.9 pad.12.own
  98.6 0.3 copy.12
  98.9 1.0 pad.13.clone
  99.9 34.9 %shard_map.69 = bf16[1,8,192,200]{3,2,1,0:T(8,128)(2,1)} custom-call(bf16[8,192,200]{2,1,0:T(8,128)(2,1)} %bitcast.31), custom_call_target="tpu_custom_call" | custom-call | tf_op jit(solution)/shard_map/pallas_call | solution.py:142
  134.8 6.0 %convolution_convert_fusion = bf16[200,2500]{1,0:T(8,128)(2,1)S(1)} fusion(bf16[1504,2500]{0,1:T(8,128)(2,1)} %param.4, bf16[1,1536,200]{2,1,0:T(8,128)(2,1)} %bitcast.34), kind=kOutput, calls=%fused_computation.2 | convolution fusion | flops 1504499968 | bytes 9462336 | tf_op jit(solution)/shard_map/dot_general | solution.py:452
  140.8 1.3 reshape.35.part
  142.2 20.8 %shard_map.70 = f32[50,2500]{1,0:T(8,128)} custom-call(bf16[4,50,2500]{2,1,0:T(8,128)(2,1)} %reshape.35.part), custom_call_target="tpu_custom_call" | custom-call | tf_op jit(solution)/shard_map/pallas_call | solution.py:420
  163.0 89.1 %shard_map.68 = (f32[752,1504]{1,0:T(8,128)}, f32[8,128]{1,0:T(8,128)}) custom-call(bf16[200,1536]{1,0:T(8,128)(2,1)} %pad.12.own, f32[8,128]{1,0:T(8,128)} %broadcast_select_fusion.stats), custom_call_target="tpu_custom_call" | custom-call | tf_op jit(solution)/shard_map/pallas_call | solution.py:367
  252.1 1.3 fusion.9
  254.8 0.0 copy-start.1
  254.8 4.8 %copy.15 = f32[752,1504]{1,0:T(8,128)} copy(f32[752,1504]{1,0:T(8,128)} %get-tuple-element.16) | data formatting | bytes 9048064
  259.6 0.0 copy-done.1
  259.6 0.8 copy.16
  (1 shorter events, 0.0 us)
Async XLA Ops:
  0.6 1.2 copy-start
  254.8 4.8 %copy-start.1 = (f32[50,2500]{1,0:T(8,128)S(1)}, f32[50,2500]{1,0:T(8,128)}, u32[]{:S(2)}) copy-start(f32[50,2500]{1,0:T(8,128)} %shard_map.70) | copy-start | bytes 1500004
